TPU v7x, 32 devices: a whole 2x2x4 slice. The times are simulated.
32 devices in a mesh: sub: 8 (over y, x, core), grp: 4 (over z).
Axes of the slice: x: 2, y: 2, z: 4, core: 2. Of those that a mesh axis runs over, the one named last changes fastest.
Arguments:
- impedance: bfloat16 [8, 4, 2048, 512], P('sub', 'grp'), may hold values from -0.125 to 0.125
- incident: bfloat16 [8, 4, 96, 512], P('sub', 'grp'), may hold values from -6 to 6
- face_order: int32 [8, 4, 192], P('sub', 'grp'), may hold values from 0 to 191, each once within a row
- near_tiles: bfloat16 [8, 4, 3, 128, 128], P('sub', 'grp'), may hold values from -0.3125 to 0.3125
- basis_right: bfloat16 [8, 4, 128, 128], P('sub', 'grp'), may hold values from -0.125 to 0.125
- rank_scale: float32 [8, 128], P('sub'), may hold values from 0.3 to 3
- rank_counts: int32 [2], replicated, may hold values from 32 to 128
- coupling: bfloat16 [8, 2, 128, 128], P('sub'), may hold values from -0.1875 to 0.1875
- basis_left: bfloat16 [8, 4, 128, 128], P('sub', 'grp'), may hold values from -0.5 to 0.5
Outputs:
- traces: bfloat16 [8, 4, 96, 512], P('sub', 'grp')
Inputs may be any that keep to these rules, and one draw needn't show every extreme that they name: `face_order`: each row is a permutation of 0 to 191.
All inputs are finite; a program needn't handle non-finite values.
Results may differ from a plain program's by a relative error of at most 0.012.
Values may be sent and summed in bfloat16 or wider, within the bound.
A program may use at most 64 MiB of HBM per device.

v0:
```python
import functools
import jax
import jax.numpy as jnp
from jax import lax
from jax.experimental import pallas as pl
from jax.experimental.pallas import tpu as pltpu
from jax.sharding import PartitionSpec as P

FACE_Q = 192
ITERS = 3


def from_partner(value, axis, distance):
    mask = 2**distance
    pairs = [(source, source ^ mask) for source in range(lax.axis_size(axis))]
    return lax.ppermute(value, axis, pairs)


def shifted(value, axis, steps):
    count = lax.axis_size(axis)
    first, last = (max(0, -steps), min(count, count - steps))
    return lax.ppermute(value, axis, [(source, source + steps) for source in range(first, last)])


def per_device(
    impedance,
    incident,
    face_order,
    near_tiles,
    basis_right,
    rank_scale,
    rank_counts,
    coupling,
    basis_left,
):
    z_cols = impedance[0, 0]
    source = incident[0, 0]
    order_map = face_order[0, 0]
    tiles = near_tiles[0, 0]
    right_basis = basis_right[0, 0]
    left_basis = basis_left[0, 0]
    couple_rows = coupling[0]
    position = lax.axis_index("sub")
    cluster = position // 4
    rank_ids = jnp.arange(rank_scale.shape[1])
    kept = jnp.where(rank_ids < rank_counts[cluster], rank_scale[0], jnp.float32(0.0))
    trace_now = source
    for sweep_index in range(ITERS):
        whole = trace_now
        for bit_number in (0, 1):
            partner = from_partner(whole, "sub", bit_number)
            upper_half = position // (1 << bit_number) % 2 == 1
            whole = jnp.where(
                upper_half,
                jnp.concatenate([partner, whole], 1),
                jnp.concatenate([whole, partner], 1),
            )
        outgoing = jnp.dot(whole, z_cols, preferred_element_type=jnp.float32).astype(jnp.bfloat16)
        lower_out = outgoing[:, :FACE_Q]
        upper_out = outgoing[:, FACE_Q : 2 * FACE_Q]
        outer_out = outgoing[:, 2 * FACE_Q :]
        partial_sum = jnp.dot(outer_out, right_basis, preferred_element_type=jnp.float32)
        total = lax.psum(partial_sum.astype(jnp.bfloat16), "grp").astype(jnp.float32)
        coefs = (total * kept).astype(jnp.bfloat16)
        block_rows = lax.all_gather(coefs[None], "sub", axis=0, tiled=True)
        sources = jnp.arange(block_rows.shape[0]) // 4
        chosen = jnp.take(couple_rows, sources, axis=0)
        chosen = jnp.where((sources != cluster)[:, None, None], chosen, jnp.zeros_like(chosen))
        far = jnp.einsum(
            "nkr,nrt->kt", block_rows, chosen, preferred_element_type=jnp.float32
        ).astype(jnp.bfloat16)
        arrived = []
        for offset in (4, -4):
            sent = (upper_out, outer_out) if offset > 0 else (lower_out, outer_out)
            arrived.append(shifted((sent[0], sent[1]), "sub", offset))
        upper_below, outer_below = arrived[0]
        lower_above, outer_above = arrived[1]
        lower_in = jnp.take(upper_below, order_map, axis=1)
        outer_in = jnp.dot(outer_out, tiles[0], preferred_element_type=jnp.float32)
        outer_in = outer_in + jnp.dot(outer_below, tiles[1], preferred_element_type=jnp.float32)
        outer_in = outer_in + jnp.dot(outer_above, tiles[2], preferred_element_type=jnp.float32)
        outer_in = outer_in + jnp.dot(far, left_basis, preferred_element_type=jnp.float32)
        joined = jnp.concatenate(
            [lower_in.astype(jnp.float32), lower_above.astype(jnp.float32), outer_in], 1
        )
        trace_now = (joined + source.astype(jnp.float32)).astype(jnp.bfloat16)
    return trace_now[None, None]


QUARTERS = 4
F32 = jnp.float32
BF16 = jnp.bfloat16


def dot(a, b):
    return jnp.dot(a, b, preferred_element_type=F32)


def two_layer_kernel(
    groups,
    z_hbm,
    inc_ref,
    order_ref,
    tiles_ref,
    right_ref,
    scale_ref,
    counts_ref,
    couple_ref,
    left_ref,
    out_ref,
    z_ref,
    inc_all,
    order_all,
    pack_all,
    all_w,
    lhs,
    base,
    mine,
    own_outer,
    other,
    plane_sum,
    other_sum,
    z_sem,
    const_send,
    const_recv,
    send,
    recv,
    far_send,
    far_recv,
):
    sub = lax.axis_index("sub")
    grp = lax.axis_index("grp")
    layer = sub // QUARTERS
    q = sub % QUARTERS
    exc, width = inc_ref.shape
    half = exc // 2
    rank = right_ref.shape[1]
    outer = tiles_ref.shape[1]
    face = order_ref.shape[1]
    upper = layer == 1
    flip0 = sub + 1 - 2 * (sub % 2)
    flip1 = sub + 2 - 4 * ((sub // 2) % 2)
    flip2 = sub + 4 - 8 * layer
    flip12 = flip1 + 4 - 8 * layer
    q1 = flip0 % QUARTERS
    q2 = flip1 % QUARTERS
    q3 = (flip1 + 1 - 2 * (flip1 % 2)) % QUARTERS

    def remote(src, dst, send_sem, recv_sem, to_sub, to_grp=None):
        return pltpu.make_async_remote_copy(
            src_ref=src,
            dst_ref=dst,
            send_sem=send_sem,
            recv_sem=recv_sem,
            device_id=(to_sub, grp if to_grp is None else to_grp),
            device_id_type=pl.DeviceIdType.MESH,
        )

    z_copies = []
    for part in range(QUARTERS):
        rows = pl.ds(part * width, width)
        copy = pltpu.make_async_copy(z_hbm.at[rows], z_ref.at[rows], z_sem.at[part])
        copy.start()
        z_copies.append(copy)

    barrier = pltpu.get_barrier_semaphore()
    greet = [(flip0, grp), (flip1, grp), (flip2, grp), (flip12, grp)]
    greet += [(flip2, lax.rem(grp + d, groups)) for d in range(1, groups)]
    for device in greet:
        pl.semaphore_signal(barrier, inc=1, device_id=device, device_id_type=pl.DeviceIdType.MESH)

    lanes = lax.broadcasted_iota(jnp.int32, (1, rank), 1)
    kept = jnp.where(lanes < counts_ref[layer], scale_ref[...], F32(0.0))
    pack_all[q, 0:outer] = (right_ref[...].astype(F32) * kept).astype(BF16)
    pack_all[q, outer : 2 * outer] = tiles_ref[0]
    pack_all[q, 2 * outer : 3 * outer] = tiles_ref[2 - layer]
    left_map = dot(couple_ref[1 - layer], left_ref[...]).astype(BF16)
    pack_all[q, 3 * outer : 3 * outer + rank] = left_map
    inc_all[q] = inc_ref[...]
    order_all[q] = order_ref[...]
    pl.semaphore_wait(barrier, len(greet))

    pending = []
    kinds = [(inc_all, inc_ref, 0), (pack_all, pack_all.at[q], 1), (order_all, order_ref, 2)]
    firsts = []
    for buf, src, i in kinds:
        a = remote(src, buf.at[q], const_send.at[i, 0], const_recv.at[i, 0], flip1)
        b = remote(src, buf.at[q], const_send.at[i, 1], const_recv.at[i, 1], flip0)
        a.start()
        b.start()
        firsts.append((a, b))
        pending += [a, b]

    def const_forward(i):
        buf = kinds[i][0]
        firsts[i][0].wait_recv()
        c = remote(buf.at[q2], buf.at[q2], const_send.at[i, 2], const_recv.at[i, 2], flip0)
        c.start()
        pending.append(c)
        return c

    for copy in z_copies:
        copy.wait()
    def z_quarter(index):
        return z_ref[pl.ds(pl.multiple_of(index * width, width), width), :]

    acc = dot(inc_ref[...], z_quarter(q))
    firsts[0][1].wait_recv()
    acc = acc + dot(inc_all[q1], z_quarter(q1))
    fwd = const_forward(0)
    acc = acc + dot(inc_all[q2], z_quarter(q2))
    fwd.wait_recv()
    acc = acc + dot(inc_all[q3], z_quarter(q3))
    base[...] = acc

    lane = lax.broadcasted_iota(jnp.int32, (half, outer), 1)
    low = lane < outer // 2
    first_here = low == upper
    first_there = low != upper
    slot = lax.broadcasted_iota(jnp.int32, (2 * outer, 2 * face), 0)
    in_half = slot % (outer // 2)
    full_entry = jnp.where(upper, slot + outer // 2, slot)
    half_entry = jnp.where(upper, in_half, in_half + outer)
    entry = jnp.where(slot < outer, full_entry, half_entry)
    along = lax.broadcasted_iota(jnp.int32, (1, face), 1)
    nothing = jnp.full((1, face), -1, jnp.int32)

    def chosen(order_row):
        below = jnp.where(upper, order_row, nothing)
        above = jnp.where(upper, nothing, along)
        wanted = jnp.concatenate([below, above], 1)
        return jnp.where(entry == wanted, F32(1.0), F32(0.0)).astype(BF16)

    def face_tiles(block):
        full = block[exc : 2 * exc]
        packed = block[2 * exc : 2 * exc + half]
        zero = jnp.zeros_like(packed)
        top = jnp.where(first_there, packed, zero)
        bottom = jnp.where(first_there, zero, packed)
        return jnp.concatenate([full, jnp.concatenate([top, bottom], 0)], 1)

    def weights():
        for part in range(QUARTERS):
            start = part * width
            z_outer = z_ref[start + 2 * face : start + width, :]
            pack = pack_all[part]
            made = dot(pack[outer:], z_outer)
            all_w[part * outer : (part + 1) * outer, :] = made[:outer].astype(BF16)
            at = (QUARTERS + 3 * part) * outer
            all_w[at : at + outer, :] = made[outer : 2 * outer].astype(BF16)
            term = made[2 * outer :]
            total = term if part == 0 else total + term
            z_face = z_ref[start : start + 2 * face, :]
            all_w[at + outer : at + 3 * outer, :] = dot(chosen(order_all[part]), z_face).astype(BF16)
        at = 4 * QUARTERS * outer
        all_w[at : at + rank, :] = total.astype(BF16)
        all_w[at + rank :, :] = jnp.zeros_like(all_w[at + rank :, :])
        lhs[:, at + rank :] = jnp.zeros_like(lhs[:, at + rank :])

    for sweep in range(ITERS):
        last = sweep == ITERS - 1
        y = acc.astype(BF16)
        outer_out = y[:, 2 * face :]
        mid = acc[:, outer : 2 * outer]
        rolled = pltpu.roll(mid, outer // 2, 1)
        mine[sweep, 0:exc] = outer_out
        mine[sweep, exc : 2 * exc] = jnp.where(upper, acc[:, 0:outer], acc[:, 2 * outer : 3 * outer]).astype(BF16)
        mine[sweep, 2 * exc : 2 * exc + half] = jnp.where(first_here, mid[:half], rolled[half:]).astype(BF16)
        own_outer[sweep, q] = outer_out

        ss, rs = send.at[sweep], recv.at[sweep]
        o_x = remote(mine.at[sweep, pl.ds(0, exc)], own_outer.at[sweep, q], ss.at[2], rs.at[2], flip1)
        o_c = remote(mine.at[sweep, pl.ds(0, exc)], own_outer.at[sweep, q], ss.at[3], rs.at[3], flip0)
        w_y = remote(mine.at[sweep], other.at[sweep, q], ss.at[0], rs.at[0], flip2)
        o_x.start()
        o_c.start()
        w_y.start()
        pending += [o_x, o_c, w_y]
        if not last:
            w_d = remote(mine.at[sweep], other.at[sweep, q], ss.at[1], rs.at[1], flip12)
            w_d.start()
            pending.append(w_d)

        if sweep == 0:
            consts = [const_forward(1), const_forward(2)]
            for i in (1, 2):
                firsts[i][1].wait_recv()
            for c in consts:
                c.wait_recv()

        o_x.wait_recv()
        o_f = remote(own_outer.at[sweep, q2], own_outer.at[sweep, q2], ss.at[4], rs.at[4], flip0)
        o_f.start()
        pending.append(o_f)
        o_c.wait_recv()
        o_f.wait_recv()
        outers = jnp.concatenate([own_outer[sweep, part] for part in range(QUARTERS)], 1)
        rights = jnp.concatenate([pack_all[part, 0:outer] for part in range(QUARTERS)], 0)
        plane_sum[sweep] = dot(outers, rights).astype(BF16)
        sums = []
        for d in range(groups):
            copy = remote(
                plane_sum.at[sweep],
                other_sum.at[sweep, d],
                far_send.at[sweep, d],
                far_recv.at[sweep, d],
                flip2,
                lax.rem(grp + d, groups),
            )
            copy.start()
            sums.append(copy)
        pending += sums

        if sweep == 0:
            weights()
        if not last:
            lhs[:, 0 : QUARTERS * outer] = outers
            w_y.wait_recv()
            y_f = remote(other.at[sweep, q], other.at[sweep, q], ss.at[5], rs.at[5], flip0)
            y_f.start()
            w_d.wait_recv()
            d_f = remote(other.at[sweep, q2], other.at[sweep, q2], ss.at[6], rs.at[6], flip0)
            d_f.start()
            pending += [y_f, d_f]
            y_f.wait_recv()
            d_f.wait_recv()
            for part in range(QUARTERS):
                at = (QUARTERS + 3 * part) * outer
                block = other[sweep, part]
                lhs[:, at : at + outer] = block[:exc]
                lhs[:, at + outer : at + 3 * outer] = face_tiles(block)
        else:
            w_y.wait_recv()
            block = other[sweep, q]
            outer_in = dot(outer_out, tiles_ref[0]) + dot(block[:exc], tiles_ref[2 - layer])
            faces = dot(face_tiles(block), chosen(order_ref[...]))
            inc = inc_ref[...].astype(F32)
            faces = faces + inc[:, : 2 * face]
            outer_in = outer_in + inc[:, 2 * face :]

        for copy in sums:
            copy.wait_recv()
        total = other_sum[sweep, 0].astype(F32)
        for d in range(1, groups):
            total = total + other_sum[sweep, d].astype(F32)
        total = total.astype(BF16)
        if not last:
            at = 4 * QUARTERS * outer
            lhs[:, at : at + rank] = total
            acc = base[...] + dot(lhs[...], all_w[...])
        else:
            outer_in = outer_in + dot(total, pack_all[q, 3 * outer : 3 * outer + rank])
            out_ref[...] = jnp.concatenate([faces, outer_in], 1).astype(BF16)
    for copy in pending:
        copy.wait_send()


def two_layers(
    groups,
    impedance,
    incident,
    face_order,
    near_tiles,
    basis_right,
    rank_scale,
    rank_counts,
    coupling,
    basis_left,
):
    order, width = impedance.shape[2:]
    exc = incident.shape[2]
    face = face_order.shape[2]
    outer = near_tiles.shape[3]
    rank = basis_right.shape[3]
    vmem = pl.BlockSpec(memory_space=pltpu.VMEM)
    dma = pltpu.SemaphoreType.DMA
    block = 2 * exc + exc // 2
    out = pl.pallas_call(
        functools.partial(two_layer_kernel, groups),
        out_shape=jax.ShapeDtypeStruct((exc, width), BF16),
        in_specs=[
            pl.BlockSpec(memory_space=pl.ANY),
            vmem,
            vmem,
            vmem,
            vmem,
            vmem,
            pl.BlockSpec(memory_space=pltpu.SMEM),
            vmem,
            vmem,
        ],
        out_specs=vmem,
        scratch_shapes=[
            pltpu.VMEM((order, width), BF16),
            pltpu.VMEM((QUARTERS, exc, width), BF16),
            pltpu.VMEM((QUARTERS, 1, face), jnp.int32),
            pltpu.VMEM((QUARTERS, 3 * outer + rank, outer), BF16),
            pltpu.VMEM((4 * QUARTERS * outer + 2 * rank, width), BF16),
            pltpu.VMEM((exc, 4 * QUARTERS * outer + 2 * rank), BF16),
            pltpu.VMEM((exc, width), F32),
            pltpu.VMEM((ITERS, block, outer), BF16),
            pltpu.VMEM((ITERS, QUARTERS, exc, outer), BF16),
            pltpu.VMEM((ITERS, QUARTERS, block, outer), BF16),
            pltpu.VMEM((ITERS, exc, rank), BF16),
            pltpu.VMEM((ITERS, groups, exc, rank), BF16),
            dma((QUARTERS,)),
            dma((3, 3)),
            dma((3, 3)),
            dma((ITERS, 7)),
            dma((ITERS, 7)),
            dma((ITERS, groups)),
            dma((ITERS, groups)),
        ],
        compiler_params=pltpu.CompilerParams(
            collective_id=0, has_side_effects=True, vmem_limit_bytes=48 * 1024 * 1024
        ),
    )(
        impedance[0, 0],
        incident[0, 0],
        face_order[0],
        near_tiles[0, 0],
        basis_right[0, 0],
        rank_scale,
        rank_counts,
        coupling[0],
        basis_left[0, 0],
    )
    return out[None, None]


def solution(mesh):
    placed = (
        P("sub", "grp", None, None),
        P("sub", "grp", None, None),
        P("sub", "grp", None),
        P("sub", "grp", None, None, None),
        P("sub", "grp", None, None),
        P("sub", None),
        P(),
        P("sub", None, None, None),
        P("sub", "grp", None, None),
    )
    two = mesh.shape["sub"] == 2 * QUARTERS
    body = functools.partial(two_layers, mesh.shape["grp"]) if two else per_device
    return jax.shard_map(
        body,
        mesh=mesh,
        in_specs=placed,
        out_specs=P("sub", "grp", None, None),
        check_vma=False,
    )
```

profile of v0, /device:TPU:0, one launch (start us, length us, event | category | flops | bytes accessed | tf_op | source)
XLA Modules:
  0.0 46.5 jit_solution(11873177086949138823)
XLA Ops:
  0.0 0.0 copy-start
  0.0 1.6 %copy-done = bf16[1,1,2048,512]{3,2,1,0:T(8,128)(2,1)S(1)} copy-done((bf16[1,1,2048,512]{3,2,1,0:T(8,128)(2,1)S(1)}, bf16[1,1,2048,512]{3,2,1,0:T(8,128)(2,1)}, u32[]{:S(2)}) %copy-start) | copy-done | bytes 2097176
  1.6 0.0 copy-start.1
  1.6 0.9 %copy-done.1 = bf16[1,1,96,512]{3,2,1,0:T(8,128)(2,1)S(1)} copy-done((bf16[1,1,96,512]{3,2,1,0:T(8,128)(2,1)S(1)}, bf16[1,1,96,512]{3,2,1,0:T(8,128)(2,1)}, u32[]{:S(2)}) %copy-start.1) | copy-done | bytes 98328
  2.5 0.0 copy-start.2
  2.5 0.9 %copy-done.2 = bf16[1,1,3,128,128]{4,3,2,1,0:T(8,128)(2,1)S(1)} copy-done((bf16[1,1,3,128,128]{4,3,2,1,0:T(8,128)(2,1)S(1)}, bf16[1,1,3,128,128]{4,3,2,1,0:T(8,128)(2,1)}, u32[]{:S(2)}) %copy-start.2) | copy-done | bytes 98328
  3.4 0.0 copy-start.3
  3.4 0.8 %copy-done.3 = bf16[1,2,128,128]{3,2,1,0:T(8,128)(2,1)S(1)} copy-done((bf16[1,2,128,128]{3,2,1,0:T(8,128)(2,1)S(1)}, bf16[1,2,128,128]{3,2,1,0:T(8,128)(2,1)}, u32[]{:S(2)}) %copy-start.3) | copy-done | bytes 65560
  4.2 0.0 copy-start.4
  4.2 0.8 %copy-done.4 = bf16[1,1,128,128]{3,2,1,0:T(8,128)(2,1)S(1)} copy-done((bf16[1,1,128,128]{3,2,1,0:T(8,128)(2,1)S(1)}, bf16[1,1,128,128]{3,2,1,0:T(8,128)(2,1)}, u32[]{:S(2)}) %copy-start.4) | copy-done | bytes 32792
  5.0 0.0 copy-start.5
  5.0 0.8 %copy-done.5 = bf16[1,1,128,128]{3,2,1,0:T(8,128)(2,1)S(1)} copy-done((bf16[1,1,128,128]{3,2,1,0:T(8,128)(2,1)S(1)}, bf16[1,1,128,128]{3,2,1,0:T(8,128)(2,1)}, u32[]{:S(2)}) %copy-start.5) | copy-done | bytes 32792
  5.7 0.0 copy-start.6
  5.7 0.7 %copy-done.6 = s32[1,1,192]{2,1,0:T(1,128)S(1)} copy-done((s32[1,1,192]{2,1,0:T(1,128)S(1)}, s32[1,1,192]{2,1,0:T(1,128)}, u32[]{:S(2)}) %copy-start.6) | copy-done | bytes 792
  6.4 0.0 copy-start.7
  6.4 0.7 %copy-done.7 = f32[1,128]{1,0:T(1,128)S(1)} copy-done((f32[1,128]{1,0:T(1,128)S(1)}, f32[1,128]{1,0:T(1,128)}, u32[]{:S(2)}) %copy-start.7) | copy-done | bytes 536
  7.1 0.0 copy-start.8
  7.1 0.7 %copy-done.8 = s32[2]{0:T(128)S(1)} copy-done((s32[2]{0:T(128)S(1)}, s32[2]{0:T(128)}, u32[]{:S(2)}) %copy-start.8) | copy-done | bytes 32
  7.7 38.1 %shard_map.91 = bf16[96,512]{1,0:T(8,128)(2,1)S(1)} custom-call(bf16[2048,512]{1,0:T(8,128)(2,1)S(1)} %bitcast.8, bf16[96,512]{1,0:T(8,128)(2,1)S(1)} %bitcast.10, s32[1,192]{1,0:T(1,128)S(1)} %bitcast.15, bf16[3,128,128]{2,1,0:T(8,128)(2,1)S(1)} %bitcast.11, bf16[128,128]{1,0:T(8,128)(2,1)S(1)} %bitcast.13, f32[1,128]{1,0:T(1,128)S(1)} %copy-done.7, ...), custom_call_target="tpu_custom_call" | custom-call | tf_op jit(solution)/shard_map/pallas_call | solution.py:378
  45.9 0.6 %copy.11 = bf16[1,1,96,512]{3,2,1,0:T(8,128)(2,1)} copy(bf16[1,1,96,512]{3,2,1,0:T(8,128)(2,1)S(1)} %bitcast.9) | data formatting | bytes 196608
Async XLA Ops:
  0.0 1.6 %copy-start = (bf16[1,1,2048,512]{3,2,1,0:T(8,128)(2,1)S(1)}, bf16[1,1,2048,512]{3,2,1,0:T(8,128)(2,1)}, u32[]{:S(2)}) copy-start(bf16[1,1,2048,512]{3,2,1,0:T(8,128)(2,1)} %param.9) | copy-start | bytes 6291460
  1.6 0.9 %copy-start.1 = (bf16[1,1,96,512]{3,2,1,0:T(8,128)(2,1)S(1)}, bf16[1,1,96,512]{3,2,1,0:T(8,128)(2,1)}, u32[]{:S(2)}) copy-start(bf16[1,1,96,512]{3,2,1,0:T(8,128)(2,1)} %param.10) | copy-start | bytes 294916
  2.5 0.9 %copy-start.2 = (bf16[1,1,3,128,128]{4,3,2,1,0:T(8,128)(2,1)S(1)}, bf16[1,1,3,128,128]{4,3,2,1,0:T(8,128)(2,1)}, u32[]{:S(2)}) copy-start(bf16[1,1,3,128,128]{4,3,2,1,0:T(8,128)(2,1)} %param.12) | copy-start | bytes 294916
  3.4 0.8 %copy-start.3 = (bf16[1,2,128,128]{3,2,1,0:T(8,128)(2,1)S(1)}, bf16[1,2,128,128]{3,2,1,0:T(8,128)(2,1)}, u32[]{:S(2)}) copy-start(bf16[1,2,128,128]{3,2,1,0:T(8,128)(2,1)} %param.16) | copy-start | bytes 196612
  4.2 0.8 %copy-start.4 = (bf16[1,1,128,128]{3,2,1,0:T(8,128)(2,1)S(1)}, bf16[1,1,128,128]{3,2,1,0:T(8,128)(2,1)}, u32[]{:S(2)}) copy-start(bf16[1,1,128,128]{3,2,1,0:T(8,128)(2,1)} %param.13) | copy-start | bytes 98308
  5.0 0.8 %copy-start.5 = (bf16[1,1,128,128]{3,2,1,0:T(8,128)(2,1)S(1)}, bf16[1,1,128,128]{3,2,1,0:T(8,128)(2,1)}, u32[]{:S(2)}) copy-start(bf16[1,1,128,128]{3,2,1,0:T(8,128)(2,1)} %param.17) | copy-start | bytes 98308
  5.7 0.7 %copy-start.6 = (s32[1,1,192]{2,1,0:T(1,128)S(1)}, s32[1,1,192]{2,1,0:T(1,128)}, u32[]{:S(2)}) copy-start(s32[1,1,192]{2,1,0:T(1,128)} %param.11) | copy-start | bytes 2308
  6.4 0.7 %copy-start.7 = (f32[1,128]{1,0:T(1,128)S(1)}, f32[1,128]{1,0:T(1,128)}, u32[]{:S(2)}) copy-start(f32[1,128]{1,0:T(1,128)} %scale_ref.1) | copy-start | bytes 1540
  7.1 0.7 %copy-start.8 = (s32[2]{0:T(128)S(1)}, s32[2]{0:T(128)}, u32[]{:S(2)}) copy-start(s32[2]{0:T(128)} %counts_ref.1) | copy-start | bytes 28
where the time goes:
time: 46.9 us; the launch traced here: 46.5 us
  Pallas kernels  38.1 us (81%)
  local copies, waits for them, and re-layouts  8.36 us (18%)
    pallas_call x1, Pallas kernels, two_layers(): pl.pallas_call(functools.partial(two_layer_kernel, groups), out_shape=jax...  38.1 us
    unnamed x19, local copies, waits for them, and re-layouts  8.36 us

commit v1 on v0

--- a/solution.py
+++ b/solution.py
@@ -99,6 +99,15 @@
 def two_layer_kernel(
     groups,
     z_hbm,
+    inc_hbm,
+    order_hbm,
+    tiles_hbm,
+    right_hbm,
+    scale_hbm,
+    counts_hbm,
+    couple_hbm,
+    left_hbm,
+    out_ref,
     inc_ref,
     order_ref,
     tiles_ref,
@@ -107,7 +116,6 @@
     counts_ref,
     couple_ref,
     left_ref,
-    out_ref,
     z_ref,
     inc_all,
     order_all,
@@ -121,6 +129,7 @@
     plane_sum,
     other_sum,
     z_sem,
+    load_sem,
     const_send,
     const_recv,
     send,
@@ -156,6 +165,21 @@
             device_id_type=pl.DeviceIdType.MESH,
         )
 
+    loads = []
+    pairs = [
+        (right_hbm, right_ref),
+        (scale_hbm, scale_ref),
+        (counts_hbm, counts_ref),
+        (tiles_hbm, tiles_ref),
+        (couple_hbm, couple_ref),
+        (left_hbm, left_ref),
+        (inc_hbm, inc_ref),
+        (order_hbm, order_ref),
+    ]
+    for i, (src, dst) in enumerate(pairs):
+        load = pltpu.make_async_copy(src, dst, load_sem.at[i])
+        load.start()
+        loads.append(load)
     z_copies = []
     for part in range(QUARTERS):
         rows = pl.ds(part * width, width)
@@ -169,6 +193,8 @@
     for device in greet:
         pl.semaphore_signal(barrier, inc=1, device_id=device, device_id_type=pl.DeviceIdType.MESH)
 
+    for load in loads:
+        load.wait()
     lanes = lax.broadcasted_iota(jnp.int32, (1, rank), 1)
     kept = jnp.where(lanes < counts_ref[layer], scale_ref[...], F32(0.0))
     pack_all[q, 0:outer] = (right_ref[...].astype(F32) * kept).astype(BF16)
@@ -378,19 +404,17 @@
     out = pl.pallas_call(
         functools.partial(two_layer_kernel, groups),
         out_shape=jax.ShapeDtypeStruct((exc, width), BF16),
-        in_specs=[
-            pl.BlockSpec(memory_space=pl.ANY),
-            vmem,
-            vmem,
-            vmem,
-            vmem,
-            vmem,
-            pl.BlockSpec(memory_space=pltpu.SMEM),
-            vmem,
-            vmem,
-        ],
+        in_specs=[pl.BlockSpec(memory_space=pltpu.HBM)] * 9,
         out_specs=vmem,
         scratch_shapes=[
+            pltpu.VMEM((exc, width), BF16),
+            pltpu.VMEM((1, face), jnp.int32),
+            pltpu.VMEM(near_tiles.shape[2:], BF16),
+            pltpu.VMEM(basis_right.shape[2:], BF16),
+            pltpu.VMEM((1, rank), F32),
+            pltpu.SMEM(rank_counts.shape, jnp.int32),
+            pltpu.VMEM(coupling.shape[1:], BF16),
+            pltpu.VMEM(basis_left.shape[2:], BF16),
             pltpu.VMEM((order, width), BF16),
             pltpu.VMEM((QUARTERS, exc, width), BF16),
             pltpu.VMEM((QUARTERS, 1, face), jnp.int32),
@@ -404,6 +428,7 @@
             pltpu.VMEM((ITERS, exc, rank), BF16),
             pltpu.VMEM((ITERS, groups, exc, rank), BF16),
             dma((QUARTERS,)),
+            dma((8,)),
             dma((3, 3)),
             dma((3, 3)),
             dma((ITERS, 7)),
@@ -415,15 +440,20 @@
             collective_id=0, has_side_effects=True, vmem_limit_bytes=48 * 1024 * 1024
         ),
     )(
-        impedance[0, 0],
-        incident[0, 0],
-        face_order[0],
-        near_tiles[0, 0],
-        basis_right[0, 0],
-        rank_scale,
-        rank_counts,
-        coupling[0],
-        basis_left[0, 0],
+        *[
+            pltpu.with_memory_space_constraint(operand, pltpu.HBM)
+            for operand in (
+                impedance[0, 0],
+                incident[0, 0],
+                face_order[0],
+                near_tiles[0, 0],
+                basis_right[0, 0],
+                rank_scale,
+                rank_counts,
+                coupling[0],
+                basis_left[0, 0],
+            )
+        ]
     )
     return out[None, None]
 

time: 46.9 us -> 38.3 us (0.82)
  local copies, waits for them, and re-layouts: 8.36 us -> 0.64 us
  Pallas kernels: 38.1 us -> 37.5 us
    unnamed x19 -> x1, local copies, waits for them, and re-layouts: 8.36 us -> 0.64 us
    pallas_call x1, Pallas kernels: 38.1 us -> 37.5 us  [two_layers(): pl.pallas_call(functools.partial(two_layer_kernel, groups), out_shape=jax...]
where the time goes in v1:
time: 38.3 us; the launch traced here: 38.1 us
  Pallas kernels  37.5 us (98%)
  local copies, waits for them, and re-layouts  0.64 us (2%)
    pallas_call x1, Pallas kernels, two_layers(): pl.pallas_call(functools.partial(two_layer_kernel, groups), out_shape=jax...  37.5 us

profile of v1, /device:TPU:0, one launch (start us, length us, event | category | flops | bytes accessed | tf_op | source)
XLA Modules:
  0.0 38.1 jit_solution(8633202711586501696)
XLA Ops:
  0.0 37.5 %shard_map.91 = bf16[96,512]{1,0:T(8,128)(2,1)S(1)} custom-call(bf16[2048,512]{1,0:T(8,128)(2,1)} %bitcast.9, bf16[96,512]{1,0:T(8,128)(2,1)} %bitcast.10, s32[1,192]{1,0:T(1,128)} %bitcast.15, bf16[3,128,128]{2,1,0:T(8,128)(2,1)} %bitcast.11, bf16[128,128]{1,0:T(8,128)(2,1)} %bitcast.13, f32[1,128]{1,0:T(1,128)} %scale_hbm.1, s32[2]{0:T(128)} %counts_hbm.1, ...), custom_call_target="tpu_custom_call" | custom-call | tf_op jit(solution)/shard_map/pallas_call | solution.py:404
  37.5 0.6 %copy.11 = bf16[1,1,96,512]{3,2,1,0:T(8,128)(2,1)} copy(bf16[1,1,96,512]{3,2,1,0:T(8,128)(2,1)S(1)} %bitcast.8) | data formatting | bytes 196608

commit v2 on v1

--- a/solution.py
+++ b/solution.py
@@ -108,8 +108,6 @@
     couple_hbm,
     left_hbm,
     out_ref,
-    inc_ref,
-    order_ref,
     tiles_ref,
     right_ref,
     scale_ref,
@@ -119,9 +117,10 @@
     z_ref,
     inc_all,
     order_all,
+    right_all,
     pack_all,
     all_w,
-    lhs,
+    g_all,
     base,
     mine,
     own_outer,
@@ -136,24 +135,30 @@
     recv,
     far_send,
     far_recv,
+    g_send,
+    g_recv,
+    slab_sem,
+    ready_sem,
+    go_sem,
 ):
     sub = lax.axis_index("sub")
     grp = lax.axis_index("grp")
     layer = sub // QUARTERS
     q = sub % QUARTERS
-    exc, width = inc_ref.shape
+    exc, width = inc_all.shape[1:]
     half = exc // 2
     rank = right_ref.shape[1]
     outer = tiles_ref.shape[1]
-    face = order_ref.shape[1]
+    face = order_all.shape[2]
     upper = layer == 1
     flip0 = sub + 1 - 2 * (sub % 2)
     flip1 = sub + 2 - 4 * ((sub // 2) % 2)
+    flip01 = flip1 + 1 - 2 * (flip1 % 2)
     flip2 = sub + 4 - 8 * layer
     flip12 = flip1 + 4 - 8 * layer
     q1 = flip0 % QUARTERS
     q2 = flip1 % QUARTERS
-    q3 = (flip1 + 1 - 2 * (flip1 % 2)) % QUARTERS
+    q3 = flip01 % QUARTERS
 
     def remote(src, dst, send_sem, recv_sem, to_sub, to_grp=None):
         return pltpu.make_async_remote_copy(
@@ -165,21 +170,28 @@
             device_id_type=pl.DeviceIdType.MESH,
         )
 
-    loads = []
-    pairs = [
-        (right_hbm, right_ref),
-        (scale_hbm, scale_ref),
-        (counts_hbm, counts_ref),
-        (tiles_hbm, tiles_ref),
-        (couple_hbm, couple_ref),
-        (left_hbm, left_ref),
-        (inc_hbm, inc_ref),
-        (order_hbm, order_ref),
-    ]
-    for i, (src, dst) in enumerate(pairs):
-        load = pltpu.make_async_copy(src, dst, load_sem.at[i])
-        load.start()
-        loads.append(load)
+    def signal(sem, to_sub, to_grp):
+        pl.semaphore_signal(
+            sem, inc=1, device_id=(to_sub, to_grp), device_id_type=pl.DeviceIdType.MESH
+        )
+
+    loads = {}
+    for i, (name, src, dst) in enumerate(
+        [
+            ("inc", inc_hbm, inc_all.at[q]),
+            ("right", right_hbm, right_ref),
+            ("scale", scale_hbm, scale_ref),
+            ("counts", counts_hbm, counts_ref),
+            ("couple", couple_hbm, couple_ref),
+            ("left", left_hbm, left_ref),
+            ("tiles", tiles_hbm, tiles_ref),
+            ("own", tiles_hbm.at[0], pack_all.at[q, pl.ds(0, outer)]),
+            ("cross", tiles_hbm.at[2 - layer], pack_all.at[q, pl.ds(outer, outer)]),
+            ("order", order_hbm, order_all.at[q]),
+        ]
+    ):
+        loads[name] = pltpu.make_async_copy(src, dst, load_sem.at[i])
+        loads[name].start()
     z_copies = []
     for part in range(QUARTERS):
         rows = pl.ds(part * width, width)
@@ -187,54 +199,90 @@
         copy.start()
         z_copies.append(copy)
 
+    slab = 2 * QUARTERS
+    lead = sub == 0
     barrier = pltpu.get_barrier_semaphore()
-    greet = [(flip0, grp), (flip1, grp), (flip2, grp), (flip12, grp)]
-    greet += [(flip2, lax.rem(grp + d, groups)) for d in range(1, groups)]
-    for device in greet:
-        pl.semaphore_signal(barrier, inc=1, device_id=device, device_id_type=pl.DeviceIdType.MESH)
-
-    for load in loads:
-        load.wait()
-    lanes = lax.broadcasted_iota(jnp.int32, (1, rank), 1)
-    kept = jnp.where(lanes < counts_ref[layer], scale_ref[...], F32(0.0))
-    pack_all[q, 0:outer] = (right_ref[...].astype(F32) * kept).astype(BF16)
-    pack_all[q, outer : 2 * outer] = tiles_ref[0]
-    pack_all[q, 2 * outer : 3 * outer] = tiles_ref[2 - layer]
-    left_map = dot(couple_ref[1 - layer], left_ref[...]).astype(BF16)
-    pack_all[q, 3 * outer : 3 * outer + rank] = left_map
-    inc_all[q] = inc_ref[...]
-    order_all[q] = order_ref[...]
-    pl.semaphore_wait(barrier, len(greet))
+
+    @pl.when(lead)
+    def _():
+        for i in range(1, slab):
+            signal(barrier, i, grp)
+        for d in range(1, groups):
+            signal(barrier, sub, lax.rem(grp + d, groups))
+
+    @pl.when(jnp.logical_not(lead))
+    def _():
+        for i in range(1, slab - 1):
+            signal(barrier, 1 + lax.rem(sub - 1 + i, slab - 1), grp)
+        pl.semaphore_wait(barrier, slab - 1)
+        signal(slab_sem, 0, grp)
+
+    @pl.when(lead)
+    def _():
+        pl.semaphore_wait(slab_sem, slab - 1)
 
     pending = []
-    kinds = [(inc_all, inc_ref, 0), (pack_all, pack_all.at[q], 1), (order_all, order_ref, 2)]
-    firsts = []
-    for buf, src, i in kinds:
-        a = remote(src, buf.at[q], const_send.at[i, 0], const_recv.at[i, 0], flip1)
-        b = remote(src, buf.at[q], const_send.at[i, 1], const_recv.at[i, 1], flip0)
+    buffers = [inc_all, right_all, pack_all, order_all]
+    firsts = {}
+
+    def const_start(i):
+        buf = buffers[i]
+        a = remote(buf.at[q], buf.at[q], const_send.at[i, 0], const_recv.at[i, 0], flip1)
+        b = remote(buf.at[q], buf.at[q], const_send.at[i, 1], const_recv.at[i, 1], flip0)
         a.start()
         b.start()
-        firsts.append((a, b))
-        pending += [a, b]
+        firsts[i] = (a, b)
+        pending.extend([a, b])
 
     def const_forward(i):
-        buf = kinds[i][0]
+        buf = buffers[i]
         firsts[i][0].wait_recv()
         c = remote(buf.at[q2], buf.at[q2], const_send.at[i, 2], const_recv.at[i, 2], flip0)
         c.start()
         pending.append(c)
         return c
 
+    loads["inc"].wait()
+    const_start(0)
+
+    for name in ("right", "scale", "counts"):
+        loads[name].wait()
+    lanes = lax.broadcasted_iota(jnp.int32, (1, rank), 1)
+    kept = jnp.where(lanes < counts_ref[layer], scale_ref[...], F32(0.0))
+    right_all[q] = (right_ref[...].astype(F32) * kept).astype(BF16)
+
+    for name in ("couple", "left", "tiles", "own", "cross", "order"):
+        loads[name].wait()
+    left_map = dot(couple_ref[1 - layer], left_ref[...]).astype(BF16)
+    pack_all[q, 2 * outer : 2 * outer + rank] = left_map
+
+    @pl.when(lead)
+    def _():
+        pl.semaphore_wait(barrier, groups - 1)
+        for d in range(1, groups):
+            signal(ready_sem, sub, lax.rem(grp + d, groups))
+
     for copy in z_copies:
         copy.wait()
+
     def z_quarter(index):
         return z_ref[pl.ds(pl.multiple_of(index * width, width), width), :]
 
-    acc = dot(inc_ref[...], z_quarter(q))
+    acc = dot(inc_all[q], z_quarter(q))
     firsts[0][1].wait_recv()
     acc = acc + dot(inc_all[q1], z_quarter(q1))
+    for i in (1, 2, 3):
+        const_start(i)
+
+    @pl.when(lead)
+    def _():
+        pl.semaphore_wait(ready_sem, groups - 1)
+        for i in range(1, slab):
+            signal(go_sem, i, grp)
+
     fwd = const_forward(0)
     acc = acc + dot(inc_all[q2], z_quarter(q2))
+    right_fwd = const_forward(1)
     fwd.wait_recv()
     acc = acc + dot(inc_all[q3], z_quarter(q3))
     base[...] = acc
@@ -250,6 +298,7 @@
     entry = jnp.where(slot < outer, full_entry, half_entry)
     along = lax.broadcasted_iota(jnp.int32, (1, face), 1)
     nothing = jnp.full((1, face), -1, jnp.int32)
+    far_at = 4 * QUARTERS * outer
 
     def chosen(order_row):
         below = jnp.where(upper, order_row, nothing)
@@ -269,8 +318,7 @@
         for part in range(QUARTERS):
             start = part * width
             z_outer = z_ref[start + 2 * face : start + width, :]
-            pack = pack_all[part]
-            made = dot(pack[outer:], z_outer)
+            made = dot(pack_all[part], z_outer)
             all_w[part * outer : (part + 1) * outer, :] = made[:outer].astype(BF16)
             at = (QUARTERS + 3 * part) * outer
             all_w[at : at + outer, :] = made[outer : 2 * outer].astype(BF16)
@@ -278,53 +326,46 @@
             total = term if part == 0 else total + term
             z_face = z_ref[start : start + 2 * face, :]
             all_w[at + outer : at + 3 * outer, :] = dot(chosen(order_all[part]), z_face).astype(BF16)
-        at = 4 * QUARTERS * outer
-        all_w[at : at + rank, :] = total.astype(BF16)
-        all_w[at + rank :, :] = jnp.zeros_like(all_w[at + rank :, :])
-        lhs[:, at + rank :] = jnp.zeros_like(lhs[:, at + rank :])
-
-    for sweep in range(ITERS):
-        last = sweep == ITERS - 1
-        y = acc.astype(BF16)
-        outer_out = y[:, 2 * face :]
+        all_w[far_at : far_at + rank, :] = total.astype(BF16)
+
+    def start_outer(sweep, outer_out):
+        own_outer[sweep, q] = outer_out
+        own_at = own_outer.at[sweep, q]
+        ss, rs = send.at[sweep], recv.at[sweep]
+        o_c = remote(own_at, own_at, ss.at[3], rs.at[3], flip0)
+        o_x = remote(own_at, own_at, ss.at[2], rs.at[2], flip1)
+        o_d = remote(own_at, own_at, ss.at[4], rs.at[4], flip01)
+        for copy in (o_d, o_x, o_c):
+            copy.start()
+            pending.append(copy)
+        return o_c, o_x, o_d
+
+    def start_near(sweep, acc):
+        ss, rs = send.at[sweep], recv.at[sweep]
         mid = acc[:, outer : 2 * outer]
         rolled = pltpu.roll(mid, outer // 2, 1)
-        mine[sweep, 0:exc] = outer_out
+        mine[sweep, 0:exc] = acc[:, 2 * face :].astype(BF16)
         mine[sweep, exc : 2 * exc] = jnp.where(upper, acc[:, 0:outer], acc[:, 2 * outer : 3 * outer]).astype(BF16)
         mine[sweep, 2 * exc : 2 * exc + half] = jnp.where(first_here, mid[:half], rolled[half:]).astype(BF16)
-        own_outer[sweep, q] = outer_out
-
-        ss, rs = send.at[sweep], recv.at[sweep]
-        o_x = remote(mine.at[sweep, pl.ds(0, exc)], own_outer.at[sweep, q], ss.at[2], rs.at[2], flip1)
-        o_c = remote(mine.at[sweep, pl.ds(0, exc)], own_outer.at[sweep, q], ss.at[3], rs.at[3], flip0)
         w_y = remote(mine.at[sweep], other.at[sweep, q], ss.at[0], rs.at[0], flip2)
-        o_x.start()
-        o_c.start()
-        w_y.start()
-        pending += [o_x, o_c, w_y]
-        if not last:
-            w_d = remote(mine.at[sweep], other.at[sweep, q], ss.at[1], rs.at[1], flip12)
-            w_d.start()
-            pending.append(w_d)
-
-        if sweep == 0:
-            consts = [const_forward(1), const_forward(2)]
-            for i in (1, 2):
-                firsts[i][1].wait_recv()
-            for c in consts:
-                c.wait_recv()
-
-        o_x.wait_recv()
-        o_f = remote(own_outer.at[sweep, q2], own_outer.at[sweep, q2], ss.at[4], rs.at[4], flip0)
-        o_f.start()
-        pending.append(o_f)
-        o_c.wait_recv()
-        o_f.wait_recv()
-        outers = jnp.concatenate([own_outer[sweep, part] for part in range(QUARTERS)], 1)
-        rights = jnp.concatenate([pack_all[part, 0:outer] for part in range(QUARTERS)], 0)
-        plane_sum[sweep] = dot(outers, rights).astype(BF16)
+        copies = [w_y]
+        if sweep < ITERS - 1:
+            copies.append(remote(mine.at[sweep], other.at[sweep, q], ss.at[1], rs.at[1], flip12))
+        for copy in copies:
+            copy.start()
+            pending.append(copy)
+        return copies
+
+    def outer_pair(sweep, first, second):
+        return dot(
+            jnp.concatenate([own_outer[sweep, first], own_outer[sweep, second]], 1),
+            jnp.concatenate([right_all[first], right_all[second]], 0),
+        )
+
+    def start_sums(sweep, value):
+        plane_sum[sweep] = value.astype(BF16)
         sums = []
-        for d in range(groups):
+        for d in sorted(range(groups), key=lambda d: -min(d, groups - d)):
             copy = remote(
                 plane_sum.at[sweep],
                 other_sum.at[sweep, d],
@@ -335,48 +376,114 @@
             )
             copy.start()
             sums.append(copy)
-        pending += sums
-
-        if sweep == 0:
-            weights()
-        if not last:
-            lhs[:, 0 : QUARTERS * outer] = outers
-            w_y.wait_recv()
-            y_f = remote(other.at[sweep, q], other.at[sweep, q], ss.at[5], rs.at[5], flip0)
-            y_f.start()
-            w_d.wait_recv()
-            d_f = remote(other.at[sweep, q2], other.at[sweep, q2], ss.at[6], rs.at[6], flip0)
-            d_f.start()
-            pending += [y_f, d_f]
-            y_f.wait_recv()
-            d_f.wait_recv()
-            for part in range(QUARTERS):
-                at = (QUARTERS + 3 * part) * outer
-                block = other[sweep, part]
-                lhs[:, at : at + outer] = block[:exc]
-                lhs[:, at + outer : at + 3 * outer] = face_tiles(block)
-        else:
-            w_y.wait_recv()
-            block = other[sweep, q]
-            outer_in = dot(outer_out, tiles_ref[0]) + dot(block[:exc], tiles_ref[2 - layer])
-            faces = dot(face_tiles(block), chosen(order_ref[...]))
-            inc = inc_ref[...].astype(F32)
-            faces = faces + inc[:, : 2 * face]
-            outer_in = outer_in + inc[:, 2 * face :]
-
+            pending.append(copy)
+        return sums
+
+    def far_total(sweep, sums):
         for copy in sums:
             copy.wait_recv()
         total = other_sum[sweep, 0].astype(F32)
         for d in range(1, groups):
             total = total + other_sum[sweep, d].astype(F32)
-        total = total.astype(BF16)
+        return total.astype(BF16)
+
+    def near_block(sweep, part):
+        block = other[sweep, part]
+        return jnp.concatenate([block[:exc], face_tiles(block)], 1)
+
+    def near_rows(part):
+        at = pl.multiple_of((QUARTERS + 3 * part) * outer, outer)
+        return all_w[pl.ds(at, 3 * outer), :]
+
+    def known_terms(sweep, w_y, w_d):
+        ss, rs = send.at[sweep], recv.at[sweep]
+        y_f = remote(other.at[sweep, q], other.at[sweep, q], ss.at[5], rs.at[5], flip0)
+        d_f = remote(other.at[sweep, q2], other.at[sweep, q2], ss.at[6], rs.at[6], flip0)
+        pending.extend([y_f, d_f])
+        outers = jnp.concatenate([own_outer[sweep, part] for part in range(QUARTERS)], 1)
+        known = base[...] + dot(outers, all_w[0 : QUARTERS * outer, :])
+        w_y.wait_recv()
+        y_f.start()
+        known = known + dot(near_block(sweep, q), near_rows(q))
+        w_d.wait_recv()
+        d_f.start()
+        known = known + dot(near_block(sweep, q2), near_rows(q2))
+        y_f.wait_recv()
+        known = known + dot(near_block(sweep, q1), near_rows(q1))
+        d_f.wait_recv()
+        block, rows = near_block(sweep, q3), near_rows(q3)
+        ahead = None
+        known_outer = known[:, 2 * face :] + dot(block, rows[:, 2 * face :])
+        if sweep == ITERS - 2:
+            ahead = start_outer(sweep + 1, known_outer.astype(BF16))
+        known_face = known[:, : 2 * face] + dot(block, rows[:, : 2 * face])
+        return jnp.concatenate([known_face, known_outer], 1), ahead
+
+    for sweep in range(ITERS):
+        last = sweep == ITERS - 1
+        if sweep == 0:
+            outs = start_outer(sweep, acc[:, 2 * face :].astype(BF16))
+            near = start_near(sweep, acc)
+            consts = [const_forward(2), const_forward(3)]
+            firsts[1][1].wait_recv()
+        elif not last:
+            near = start_near(sweep, acc)
+            outs = start_outer(sweep, acc[:, 2 * face :].astype(BF16))
+        else:
+            near = start_near(sweep, acc)
+            outs = ahead
+        outs[0].wait_recv()
+        value = outer_pair(sweep, q, q1)
+        if last:
+            for copy in shares:
+                copy.wait_recv()
+            whole = g_all[0].astype(F32)
+            for part in range(1, QUARTERS):
+                whole = whole + g_all[part].astype(F32)
+            value = value + dot(total, whole.astype(BF16))
+        if sweep == 0:
+            right_fwd.wait_recv()
+        outs[1].wait_recv()
+        outs[2].wait_recv()
+        value = value + outer_pair(sweep, q2, q3)
+        if sweep == 0:
+
+            @pl.when(jnp.logical_not(lead))
+            def _():
+                pl.semaphore_wait(go_sem, 1)
+
+        sums = start_sums(sweep, value)
+        if sweep == 0:
+            for i in (2, 3):
+                firsts[i][1].wait_recv()
+            for c in consts:
+                c.wait_recv()
+            weights()
+            far_outer = all_w[far_at : far_at + rank, 2 * face :]
+            g_all[q] = dot(far_outer, right_all[q]).astype(BF16)
+            shares = [
+                remote(g_all.at[q], g_all.at[q], g_send.at[i], g_recv.at[i], peer)
+                for i, peer in enumerate((flip01, flip1, flip0))
+            ]
+            for copy in shares:
+                copy.start()
+                pending.append(copy)
         if not last:
-            at = 4 * QUARTERS * outer
-            lhs[:, at : at + rank] = total
-            acc = base[...] + dot(lhs[...], all_w[...])
+            known, ahead = known_terms(sweep, *near)
+            total = far_total(sweep, sums)
+            acc = known + dot(total, all_w[far_at : far_at + rank, :])
         else:
-            outer_in = outer_in + dot(total, pack_all[q, 3 * outer : 3 * outer + rank])
-            out_ref[...] = jnp.concatenate([faces, outer_in], 1).astype(BF16)
+            near[0].wait_recv()
+            block = other[sweep, q]
+            outer_in = dot(acc[:, 2 * face :].astype(BF16), tiles_ref[0])
+            outer_in = outer_in + dot(block[:exc], tiles_ref[2 - layer])
+            faces = dot(face_tiles(block), chosen(order_all[q]))
+            inc = inc_all[q].astype(F32)
+            out_ref[:, 0 : 2 * face] = (faces + inc[:, : 2 * face]).astype(BF16)
+            outer_in = outer_in + inc[:, 2 * face :]
+            total = far_total(sweep, sums)
+            outer_in = outer_in + dot(total, pack_all[q, 2 * outer : 2 * outer + rank])
+            out_ref[:, 2 * face :] = outer_in.astype(BF16)
     for copy in pending:
         copy.wait_send()
 
@@ -407,8 +514,6 @@
         in_specs=[pl.BlockSpec(memory_space=pltpu.HBM)] * 9,
         out_specs=vmem,
         scratch_shapes=[
-            pltpu.VMEM((exc, width), BF16),
-            pltpu.VMEM((1, face), jnp.int32),
             pltpu.VMEM(near_tiles.shape[2:], BF16),
             pltpu.VMEM(basis_right.shape[2:], BF16),
             pltpu.VMEM((1, rank), F32),
@@ -418,9 +523,10 @@
             pltpu.VMEM((order, width), BF16),
             pltpu.VMEM((QUARTERS, exc, width), BF16),
             pltpu.VMEM((QUARTERS, 1, face), jnp.int32),
-            pltpu.VMEM((QUARTERS, 3 * outer + rank, outer), BF16),
-            pltpu.VMEM((4 * QUARTERS * outer + 2 * rank, width), BF16),
-            pltpu.VMEM((exc, 4 * QUARTERS * outer + 2 * rank), BF16),
+            pltpu.VMEM((QUARTERS, outer, rank), BF16),
+            pltpu.VMEM((QUARTERS, 2 * outer + rank, outer), BF16),
+            pltpu.VMEM((4 * QUARTERS * outer + rank, width), BF16),
+            pltpu.VMEM((QUARTERS, rank, rank), BF16),
             pltpu.VMEM((exc, width), F32),
             pltpu.VMEM((ITERS, block, outer), BF16),
             pltpu.VMEM((ITERS, QUARTERS, exc, outer), BF16),
@@ -428,13 +534,18 @@
             pltpu.VMEM((ITERS, exc, rank), BF16),
             pltpu.VMEM((ITERS, groups, exc, rank), BF16),
             dma((QUARTERS,)),
-            dma((8,)),
-            dma((3, 3)),
-            dma((3, 3)),
+            dma((10,)),
+            dma((4, 3)),
+            dma((4, 3)),
             dma((ITERS, 7)),
             dma((ITERS, 7)),
             dma((ITERS, groups)),
             dma((ITERS, groups)),
+            dma((3,)),
+            dma((3,)),
+            pltpu.SemaphoreType.REGULAR,
+            pltpu.SemaphoreType.REGULAR,
+            pltpu.SemaphoreType.REGULAR,
         ],
         compiler_params=pltpu.CompilerParams(
             collective_id=0, has_side_effects=True, vmem_limit_bytes=48 * 1024 * 1024

time: 38.3 us -> 35.3 us (0.922)
  Pallas kernels: 37.5 us -> 34.5 us
    pallas_call x1, Pallas kernels: 37.5 us -> 34.5 us  [two_layers(): pl.pallas_call(functools.partial(two_layer_kernel, groups), out_shape=jax...]
where the time goes in v2:
time: 35.3 us; the launch traced here: 35.1 us
  Pallas kernels  34.5 us (98%)
  local copies, waits for them, and re-layouts  0.64 us (2%)
    pallas_call x1, Pallas kernels, two_layers(): pl.pallas_call(functools.partial(two_layer_kernel, groups), out_shape=jax...  34.5 us

profile of v2, /device:TPU:0, one launch (start us, length us, event | category | flops | bytes accessed | tf_op | source)
XLA Modules:
  0.0 35.1 jit_solution(15668899694732748651)
XLA Ops:
  0.0 34.5 %shard_map.91 = bf16[96,512]{1,0:T(8,128)(2,1)S(1)} custom-call(bf16[2048,512]{1,0:T(8,128)(2,1)} %bitcast.9, bf16[96,512]{1,0:T(8,128)(2,1)} %bitcast.10, s32[1,192]{1,0:T(1,128)} %bitcast.15, bf16[3,128,128]{2,1,0:T(8,128)(2,1)} %bitcast.11, bf16[128,128]{1,0:T(8,128)(2,1)} %bitcast.13, f32[1,128]{1,0:T(1,128)} %scale_hbm.1, s32[2]{0:T(128)} %counts_hbm.1, ...), custom_call_target="tpu_custom_call" | custom-call | tf_op jit(solution)/shard_map/pallas_call | solution.py:511
  34.5 0.6 %copy.11 = bf16[1,1,96,512]{3,2,1,0:T(8,128)(2,1)} copy(bf16[1,1,96,512]{3,2,1,0:T(8,128)(2,1)S(1)} %bitcast.8) | data formatting | bytes 196608

commit v3 on v2

--- a/solution.py
+++ b/solution.py
@@ -108,7 +108,9 @@
     couple_hbm,
     left_hbm,
     out_ref,
-    tiles_ref,
+    own_ref,
+    cross_ref,
+    cross_there,
     right_ref,
     scale_ref,
     counts_ref,
@@ -117,13 +119,13 @@
     z_ref,
     inc_all,
     order_all,
-    right_all,
-    pack_all,
+    left_all,
     all_w,
     g_all,
     base,
     mine,
-    own_outer,
+    sourced,
+    owned,
     other,
     plane_sum,
     other_sum,
@@ -137,6 +139,8 @@
     far_recv,
     g_send,
     g_recv,
+    cross_send,
+    cross_recv,
     slab_sem,
     ready_sem,
     go_sem,
@@ -148,7 +152,7 @@
     exc, width = inc_all.shape[1:]
     half = exc // 2
     rank = right_ref.shape[1]
-    outer = tiles_ref.shape[1]
+    outer = own_ref.shape[1]
     face = order_all.shape[2]
     upper = layer == 1
     flip0 = sub + 1 - 2 * (sub % 2)
@@ -184,9 +188,8 @@
             ("counts", counts_hbm, counts_ref),
             ("couple", couple_hbm, couple_ref),
             ("left", left_hbm, left_ref),
-            ("tiles", tiles_hbm, tiles_ref),
-            ("own", tiles_hbm.at[0], pack_all.at[q, pl.ds(0, outer)]),
-            ("cross", tiles_hbm.at[2 - layer], pack_all.at[q, pl.ds(outer, outer)]),
+            ("own", tiles_hbm.at[0], own_ref),
+            ("cross", tiles_hbm.at[2 - layer], cross_ref),
             ("order", order_hbm, order_all.at[q]),
         ]
     ):
@@ -222,7 +225,7 @@
         pl.semaphore_wait(slab_sem, slab - 1)
 
     pending = []
-    buffers = [inc_all, right_all, pack_all, order_all]
+    buffers = [inc_all, left_all, order_all]
     firsts = {}
 
     def const_start(i):
@@ -245,16 +248,16 @@
     loads["inc"].wait()
     const_start(0)
 
-    for name in ("right", "scale", "counts"):
+    loads["cross"].wait()
+    cross_copy = remote(cross_ref, cross_there, cross_send, cross_recv, flip2)
+    cross_copy.start()
+    pending.append(cross_copy)
+    for name in ("right", "scale", "counts", "couple", "left", "own", "order"):
         loads[name].wait()
     lanes = lax.broadcasted_iota(jnp.int32, (1, rank), 1)
     kept = jnp.where(lanes < counts_ref[layer], scale_ref[...], F32(0.0))
-    right_all[q] = (right_ref[...].astype(F32) * kept).astype(BF16)
-
-    for name in ("couple", "left", "tiles", "own", "cross", "order"):
-        loads[name].wait()
-    left_map = dot(couple_ref[1 - layer], left_ref[...]).astype(BF16)
-    pack_all[q, 2 * outer : 2 * outer + rank] = left_map
+    right_ref[...] = (right_ref[...].astype(F32) * kept).astype(BF16)
+    left_all[q] = dot(couple_ref[1 - layer], left_ref[...]).astype(BF16)
 
     @pl.when(lead)
     def _():
@@ -271,7 +274,7 @@
     acc = dot(inc_all[q], z_quarter(q))
     firsts[0][1].wait_recv()
     acc = acc + dot(inc_all[q1], z_quarter(q1))
-    for i in (1, 2, 3):
+    for i in (1, 2):
         const_start(i)
 
     @pl.when(lead)
@@ -282,7 +285,6 @@
 
     fwd = const_forward(0)
     acc = acc + dot(inc_all[q2], z_quarter(q2))
-    right_fwd = const_forward(1)
     fwd.wait_recv()
     acc = acc + dot(inc_all[q3], z_quarter(q3))
     base[...] = acc
@@ -298,7 +300,7 @@
     entry = jnp.where(slot < outer, full_entry, half_entry)
     along = lax.broadcasted_iota(jnp.int32, (1, face), 1)
     nothing = jnp.full((1, face), -1, jnp.int32)
-    far_at = 4 * QUARTERS * outer
+    far_at = 3 * QUARTERS * outer
 
     def chosen(order_row):
         below = jnp.where(upper, order_row, nothing)
@@ -316,35 +318,54 @@
 
     def weights():
         for part in range(QUARTERS):
-            start = part * width
+            start, at = part * width, 3 * part * outer
             z_outer = z_ref[start + 2 * face : start + width, :]
-            made = dot(pack_all[part], z_outer)
-            all_w[part * outer : (part + 1) * outer, :] = made[:outer].astype(BF16)
-            at = (QUARTERS + 3 * part) * outer
-            all_w[at : at + outer, :] = made[outer : 2 * outer].astype(BF16)
-            term = made[2 * outer :]
+            all_w[at : at + outer, :] = z_outer
+            term = dot(left_all[part], z_outer)
             total = term if part == 0 else total + term
             z_face = z_ref[start : start + 2 * face, :]
             all_w[at + outer : at + 3 * outer, :] = dot(chosen(order_all[part]), z_face).astype(BF16)
         all_w[far_at : far_at + rank, :] = total.astype(BF16)
 
-    def start_outer(sweep, outer_out):
-        own_outer[sweep, q] = outer_out
-        own_at = own_outer.at[sweep, q]
+    def to_plane(buf, sweep, first_sem, value):
+        buf[sweep, q] = value.astype(BF16)
+        at = buf.at[sweep, q]
+        copies = []
+        for sem, peer in ((first_sem, flip01), (first_sem + 1, flip1), (first_sem + 2, flip0)):
+            copy = remote(at, at, send.at[sweep, sem], recv.at[sweep, sem], peer)
+            copy.start()
+            copies.append(copy)
+            pending.append(copy)
+        return copies[::-1]
+
+    def start_source(sweep, outer_out):
+        return to_plane(sourced, sweep, 2, dot(outer_out, right_ref[...]))
+
+    def start_own(sweep, outer_out):
+        owned[sweep, q] = dot(outer_out, own_ref[...]).astype(BF16)
+        at = owned.at[sweep, q]
         ss, rs = send.at[sweep], recv.at[sweep]
-        o_c = remote(own_at, own_at, ss.at[3], rs.at[3], flip0)
-        o_x = remote(own_at, own_at, ss.at[2], rs.at[2], flip1)
-        o_d = remote(own_at, own_at, ss.at[4], rs.at[4], flip01)
-        for copy in (o_d, o_x, o_c):
-            copy.start()
-            pending.append(copy)
-        return o_c, o_x, o_d
+        v_x = remote(at, at, ss.at[8], rs.at[8], flip1)
+        v_c = remote(at, at, ss.at[9], rs.at[9], flip0)
+        v_x.start()
+        v_c.start()
+        pending.extend([v_x, v_c])
+        return v_c, v_x
+
+    def forward_own(sweep, own):
+        own[1].wait_recv()
+        at = owned.at[sweep, q2]
+        v_f = remote(at, at, send.at[sweep, 7], recv.at[sweep, 7], flip0)
+        v_f.start()
+        pending.append(v_f)
+        return v_f
 
     def start_near(sweep, acc):
         ss, rs = send.at[sweep], recv.at[sweep]
         mid = acc[:, outer : 2 * outer]
         rolled = pltpu.roll(mid, outer // 2, 1)
-        mine[sweep, 0:exc] = acc[:, 2 * face :].astype(BF16)
+        crossed = dot(acc[:, 2 * face :].astype(BF16), cross_there[...])
+        mine[sweep, 0:exc] = crossed.astype(BF16)
         mine[sweep, exc : 2 * exc] = jnp.where(upper, acc[:, 0:outer], acc[:, 2 * outer : 3 * outer]).astype(BF16)
         mine[sweep, 2 * exc : 2 * exc + half] = jnp.where(first_here, mid[:half], rolled[half:]).astype(BF16)
         w_y = remote(mine.at[sweep], other.at[sweep, q], ss.at[0], rs.at[0], flip2)
@@ -355,12 +376,6 @@
             copy.start()
             pending.append(copy)
         return copies
-
-    def outer_pair(sweep, first, second):
-        return dot(
-            jnp.concatenate([own_outer[sweep, first], own_outer[sweep, second]], 1),
-            jnp.concatenate([right_all[first], right_all[second]], 0),
-        )
 
     def start_sums(sweep, value):
         plane_sum[sweep] = value.astype(BF16)
@@ -389,63 +404,67 @@
 
     def near_block(sweep, part):
         block = other[sweep, part]
-        return jnp.concatenate([block[:exc], face_tiles(block)], 1)
+        outer_in = owned[sweep, part].astype(F32) + block[:exc].astype(F32)
+        return jnp.concatenate([outer_in.astype(BF16), face_tiles(block)], 1)
 
     def near_rows(part):
-        at = pl.multiple_of((QUARTERS + 3 * part) * outer, outer)
+        at = pl.multiple_of(3 * part * outer, outer)
         return all_w[pl.ds(at, 3 * outer), :]
 
-    def known_terms(sweep, w_y, w_d):
+    def known_terms(sweep, near, own):
+        w_y, w_d = near
         ss, rs = send.at[sweep], recv.at[sweep]
         y_f = remote(other.at[sweep, q], other.at[sweep, q], ss.at[5], rs.at[5], flip0)
         d_f = remote(other.at[sweep, q2], other.at[sweep, q2], ss.at[6], rs.at[6], flip0)
         pending.extend([y_f, d_f])
-        outers = jnp.concatenate([own_outer[sweep, part] for part in range(QUARTERS)], 1)
-        known = base[...] + dot(outers, all_w[0 : QUARTERS * outer, :])
         w_y.wait_recv()
         y_f.start()
-        known = known + dot(near_block(sweep, q), near_rows(q))
+        v_f = forward_own(sweep, own)
+        known = base[...] + dot(near_block(sweep, q), near_rows(q))
         w_d.wait_recv()
         d_f.start()
         known = known + dot(near_block(sweep, q2), near_rows(q2))
+        own[0].wait_recv()
         y_f.wait_recv()
         known = known + dot(near_block(sweep, q1), near_rows(q1))
+        v_f.wait_recv()
         d_f.wait_recv()
         block, rows = near_block(sweep, q3), near_rows(q3)
+        known_outer = known[:, 2 * face :] + dot(block, rows[:, 2 * face :])
         ahead = None
-        known_outer = known[:, 2 * face :] + dot(block, rows[:, 2 * face :])
         if sweep == ITERS - 2:
-            ahead = start_outer(sweep + 1, known_outer.astype(BF16))
+            ahead = start_source(sweep + 1, known_outer.astype(BF16))
         known_face = known[:, : 2 * face] + dot(block, rows[:, : 2 * face])
         return jnp.concatenate([known_face, known_outer], 1), ahead
 
     for sweep in range(ITERS):
         last = sweep == ITERS - 1
+        outer_out = acc[:, 2 * face :].astype(BF16)
         if sweep == 0:
-            outs = start_outer(sweep, acc[:, 2 * face :].astype(BF16))
+            outs = start_source(sweep, outer_out)
+            cross_copy.wait_recv()
             near = start_near(sweep, acc)
-            consts = [const_forward(2), const_forward(3)]
-            firsts[1][1].wait_recv()
+            own = start_own(sweep, outer_out)
+            consts = [const_forward(1), const_forward(2)]
         elif not last:
             near = start_near(sweep, acc)
-            outs = start_outer(sweep, acc[:, 2 * face :].astype(BF16))
+            outs = start_source(sweep, outer_out)
+            own = start_own(sweep, outer_out)
         else:
             near = start_near(sweep, acc)
             outs = ahead
-        outs[0].wait_recv()
-        value = outer_pair(sweep, q, q1)
         if last:
             for copy in shares:
                 copy.wait_recv()
             whole = g_all[0].astype(F32)
             for part in range(1, QUARTERS):
                 whole = whole + g_all[part].astype(F32)
-            value = value + dot(total, whole.astype(BF16))
-        if sweep == 0:
-            right_fwd.wait_recv()
-        outs[1].wait_recv()
-        outs[2].wait_recv()
-        value = value + outer_pair(sweep, q2, q3)
+            value = dot(total, whole.astype(BF16))
+        for copy in outs:
+            copy.wait_recv()
+        for part in range(QUARTERS):
+            term = sourced[sweep, part].astype(F32)
+            value = value + term if last or part else term
         if sweep == 0:
 
             @pl.when(jnp.logical_not(lead))
@@ -454,13 +473,13 @@
 
         sums = start_sums(sweep, value)
         if sweep == 0:
-            for i in (2, 3):
+            for i in (1, 2):
                 firsts[i][1].wait_recv()
             for c in consts:
                 c.wait_recv()
             weights()
             far_outer = all_w[far_at : far_at + rank, 2 * face :]
-            g_all[q] = dot(far_outer, right_all[q]).astype(BF16)
+            g_all[q] = dot(far_outer, right_ref[...]).astype(BF16)
             shares = [
                 remote(g_all.at[q], g_all.at[q], g_send.at[i], g_recv.at[i], peer)
                 for i, peer in enumerate((flip01, flip1, flip0))
@@ -469,20 +488,19 @@
                 copy.start()
                 pending.append(copy)
         if not last:
-            known, ahead = known_terms(sweep, *near)
+            known, ahead = known_terms(sweep, near, own)
             total = far_total(sweep, sums)
             acc = known + dot(total, all_w[far_at : far_at + rank, :])
         else:
             near[0].wait_recv()
             block = other[sweep, q]
-            outer_in = dot(acc[:, 2 * face :].astype(BF16), tiles_ref[0])
-            outer_in = outer_in + dot(block[:exc], tiles_ref[2 - layer])
+            outer_in = dot(outer_out, own_ref[...]) + block[:exc].astype(F32)
             faces = dot(face_tiles(block), chosen(order_all[q]))
             inc = inc_all[q].astype(F32)
             out_ref[:, 0 : 2 * face] = (faces + inc[:, : 2 * face]).astype(BF16)
             outer_in = outer_in + inc[:, 2 * face :]
             total = far_total(sweep, sums)
-            outer_in = outer_in + dot(total, pack_all[q, 2 * outer : 2 * outer + rank])
+            outer_in = outer_in + dot(total, left_all[q])
             out_ref[:, 2 * face :] = outer_in.astype(BF16)
     for copy in pending:
         copy.wait_send()
@@ -514,35 +532,39 @@
         in_specs=[pl.BlockSpec(memory_space=pltpu.HBM)] * 9,
         out_specs=vmem,
         scratch_shapes=[
-            pltpu.VMEM(near_tiles.shape[2:], BF16),
-            pltpu.VMEM(basis_right.shape[2:], BF16),
+            pltpu.VMEM((outer, outer), BF16),
+            pltpu.VMEM((outer, outer), BF16),
+            pltpu.VMEM((outer, outer), BF16),
+            pltpu.VMEM((outer, rank), BF16),
             pltpu.VMEM((1, rank), F32),
             pltpu.SMEM(rank_counts.shape, jnp.int32),
             pltpu.VMEM(coupling.shape[1:], BF16),
-            pltpu.VMEM(basis_left.shape[2:], BF16),
+            pltpu.VMEM((rank, outer), BF16),
             pltpu.VMEM((order, width), BF16),
             pltpu.VMEM((QUARTERS, exc, width), BF16),
             pltpu.VMEM((QUARTERS, 1, face), jnp.int32),
-            pltpu.VMEM((QUARTERS, outer, rank), BF16),
-            pltpu.VMEM((QUARTERS, 2 * outer + rank, outer), BF16),
-            pltpu.VMEM((4 * QUARTERS * outer + rank, width), BF16),
+            pltpu.VMEM((QUARTERS, rank, outer), BF16),
+            pltpu.VMEM((3 * QUARTERS * outer + rank, width), BF16),
             pltpu.VMEM((QUARTERS, rank, rank), BF16),
             pltpu.VMEM((exc, width), F32),
             pltpu.VMEM((ITERS, block, outer), BF16),
+            pltpu.VMEM((ITERS, QUARTERS, exc, rank), BF16),
             pltpu.VMEM((ITERS, QUARTERS, exc, outer), BF16),
             pltpu.VMEM((ITERS, QUARTERS, block, outer), BF16),
             pltpu.VMEM((ITERS, exc, rank), BF16),
             pltpu.VMEM((ITERS, groups, exc, rank), BF16),
             dma((QUARTERS,)),
-            dma((10,)),
-            dma((4, 3)),
-            dma((4, 3)),
-            dma((ITERS, 7)),
-            dma((ITERS, 7)),
+            dma((9,)),
+            dma((3, 3)),
+            dma((3, 3)),
+            dma((ITERS, 10)),
+            dma((ITERS, 10)),
             dma((ITERS, groups)),
             dma((ITERS, groups)),
             dma((3,)),
             dma((3,)),
+            dma,
+            dma,
             pltpu.SemaphoreType.REGULAR,
             pltpu.SemaphoreType.REGULAR,
             pltpu.SemaphoreType.REGULAR,

time: 35.3 us -> 35 us (level)
  no operation moved by 1% of the time
where the time goes in v3:
time: 35 us; the launch traced here: 34.8 us
  Pallas kernels  34.2 us (98%)
  local copies, waits for them, and re-layouts  0.64 us (2%)
    pallas_call x1, Pallas kernels, two_layers(): pl.pallas_call(functools.partial(two_layer_kernel, groups), out_shape=jax...  34.2 us

profile of v3, /device:TPU:0, one launch (start us, length us, event | category | flops | bytes accessed | tf_op | source)
XLA Modules:
  0.0 34.8 jit_solution(5746770775077716489)
XLA Ops:
  0.0 34.2 %shard_map.91 = bf16[96,512]{1,0:T(8,128)(2,1)S(1)} custom-call(bf16[2048,512]{1,0:T(8,128)(2,1)} %bitcast.9, bf16[96,512]{1,0:T(8,128)(2,1)} %bitcast.10, s32[1,192]{1,0:T(1,128)} %bitcast.15, bf16[3,128,128]{2,1,0:T(8,128)(2,1)} %bitcast.11, bf16[128,128]{1,0:T(8,128)(2,1)} %bitcast.13, f32[1,128]{1,0:T(1,128)} %scale_hbm.1, s32[2]{0:T(128)} %counts_hbm.1, ...), custom_call_target="tpu_custom_call" | custom-call | tf_op jit(solution)/shard_map/pallas_call | solution.py:529
  34.2 0.6 %copy.11 = bf16[1,1,96,512]{3,2,1,0:T(8,128)(2,1)} copy(bf16[1,1,96,512]{3,2,1,0:T(8,128)(2,1)S(1)} %bitcast.8) | data formatting | bytes 196608

commit v4 on v3

--- a/solution.py
+++ b/solution.py
@@ -246,7 +246,16 @@
         return c
 
     loads["inc"].wait()
-    const_start(0)
+    cut = exc * 1 // 2 // 16 * 16
+    head = inc_all.at[q, pl.ds(0, cut)]
+    tail = inc_all.at[q, pl.ds(cut, exc - cut)]
+    inc_x = remote(head, head, const_send.at[0, 0], const_recv.at[0, 0], flip1)
+    inc_c = remote(inc_all.at[q], inc_all.at[q], const_send.at[0, 1], const_recv.at[0, 1], flip0)
+    inc_tx = remote(tail, tail, const_send.at[3, 0], const_recv.at[3, 0], flip1)
+    inc_td = remote(tail, tail, const_send.at[3, 1], const_recv.at[3, 1], flip01)
+    for copy in (inc_x, inc_c, inc_td, inc_tx):
+        copy.start()
+        pending.append(copy)
 
     loads["cross"].wait()
     cross_copy = remote(cross_ref, cross_there, cross_send, cross_recv, flip2)
@@ -272,7 +281,7 @@
         return z_ref[pl.ds(pl.multiple_of(index * width, width), width), :]
 
     acc = dot(inc_all[q], z_quarter(q))
-    firsts[0][1].wait_recv()
+    inc_c.wait_recv()
     acc = acc + dot(inc_all[q1], z_quarter(q1))
     for i in (1, 2):
         const_start(i)
@@ -283,8 +292,14 @@
         for i in range(1, slab):
             signal(go_sem, i, grp)
 
-    fwd = const_forward(0)
+    inc_x.wait_recv()
+    moved = inc_all.at[q2, pl.ds(0, cut)]
+    fwd = remote(moved, moved, const_send.at[0, 2], const_recv.at[0, 2], flip0)
+    fwd.start()
+    pending.append(fwd)
+    inc_tx.wait_recv()
     acc = acc + dot(inc_all[q2], z_quarter(q2))
+    inc_td.wait_recv()
     fwd.wait_recv()
     acc = acc + dot(inc_all[q3], z_quarter(q3))
     base[...] = acc
@@ -555,8 +570,8 @@
             pltpu.VMEM((ITERS, groups, exc, rank), BF16),
             dma((QUARTERS,)),
             dma((9,)),
-            dma((3, 3)),
-            dma((3, 3)),
+            dma((4, 3)),
+            dma((4, 3)),
             dma((ITERS, 10)),
             dma((ITERS, 10)),
             dma((ITERS, groups)),

time: 35 us -> 34.4 us (0.983)
  Pallas kernels: 34.2 us -> 33.6 us
    pallas_call x1, Pallas kernels: 34.2 us -> 33.6 us  [two_layers(): pl.pallas_call(functools.partial(two_layer_kernel, groups), out_shape=jax...]
where the time goes in v4:
time: 34.4 us; the launch traced here: 34.3 us
  Pallas kernels  33.6 us (98%)
  local copies, waits for them, and re-layouts  0.64 us (2%)
    pallas_call x1, Pallas kernels, two_layers(): pl.pallas_call(functools.partial(two_layer_kernel, groups), out_shape=jax...  33.6 us

profile of v4, /device:TPU:0, one launch (start us, length us, event | category | flops | bytes accessed | tf_op | source)
XLA Modules:
  0.0 34.3 jit_solution(5854130845732932946)
XLA Ops:
  0.0 33.6 %shard_map.91 = bf16[96,512]{1,0:T(8,128)(2,1)S(1)} custom-call(bf16[2048,512]{1,0:T(8,128)(2,1)} %bitcast.9, bf16[96,512]{1,0:T(8,128)(2,1)} %bitcast.10, s32[1,192]{1,0:T(1,128)} %bitcast.15, bf16[3,128,128]{2,1,0:T(8,128)(2,1)} %bitcast.11, bf16[128,128]{1,0:T(8,128)(2,1)} %bitcast.13, f32[1,128]{1,0:T(1,128)} %scale_hbm.1, s32[2]{0:T(128)} %counts_hbm.1, ...), custom_call_target="tpu_custom_call" | custom-call | tf_op jit(solution)/shard_map/pallas_call | solution.py:544
  33.7 0.6 %copy.11 = bf16[1,1,96,512]{3,2,1,0:T(8,128)(2,1)} copy(bf16[1,1,96,512]{3,2,1,0:T(8,128)(2,1)S(1)} %bitcast.8) | data formatting | bytes 196608

commit v5 on v4

--- a/solution.py
+++ b/solution.py
@@ -395,7 +395,7 @@
     def start_sums(sweep, value):
         plane_sum[sweep] = value.astype(BF16)
         sums = []
-        for d in sorted(range(groups), key=lambda d: -min(d, groups - d)):
+        for d in range(groups - 1, -1, -1):
             copy = remote(
                 plane_sum.at[sweep],
                 other_sum.at[sweep, d],
@@ -462,8 +462,8 @@
             own = start_own(sweep, outer_out)
             consts = [const_forward(1), const_forward(2)]
         elif not last:
+            outs = start_source(sweep, outer_out)
             near = start_near(sweep, acc)
-            outs = start_source(sweep, outer_out)
             own = start_own(sweep, outer_out)
         else:
             near = start_near(sweep, acc)

time: 34.4 us -> 34.4 us (level)
  no operation moved by 1% of the time
where the time goes in v5:
time: 34.4 us; the launch traced here: 34.3 us
  Pallas kernels  33.6 us (98%)
  local copies, waits for them, and re-layouts  0.64 us (2%)
    pallas_call x1, Pallas kernels, two_layers(): pl.pallas_call(functools.partial(two_layer_kernel, groups), out_shape=jax...  33.6 us

profile of v5, /device:TPU:0, one launch (start us, length us, event | category | flops | bytes accessed | tf_op | source)
XLA Modules:
  0.0 34.3 jit_solution(7097996940484651793)
XLA Ops:
  0.0 33.6 %shard_map.91 = bf16[96,512]{1,0:T(8,128)(2,1)S(1)} custom-call(bf16[2048,512]{1,0:T(8,128)(2,1)} %bitcast.9, bf16[96,512]{1,0:T(8,128)(2,1)} %bitcast.10, s32[1,192]{1,0:T(1,128)} %bitcast.15, bf16[3,128,128]{2,1,0:T(8,128)(2,1)} %bitcast.11, bf16[128,128]{1,0:T(8,128)(2,1)} %bitcast.13, f32[1,128]{1,0:T(1,128)} %scale_hbm.1, s32[2]{0:T(128)} %counts_hbm.1, ...), custom_call_target="tpu_custom_call" | custom-call | tf_op jit(solution)/shard_map/pallas_call | solution.py:544
  33.6 0.6 %copy.11 = bf16[1,1,96,512]{3,2,1,0:T(8,128)(2,1)} copy(bf16[1,1,96,512]{3,2,1,0:T(8,128)(2,1)S(1)} %bitcast.8) | data formatting | bytes 196608

commit v6 on v5

--- a/solution.py
+++ b/solution.py
@@ -457,9 +457,9 @@
         outer_out = acc[:, 2 * face :].astype(BF16)
         if sweep == 0:
             outs = start_source(sweep, outer_out)
+            own = start_own(sweep, outer_out)
             cross_copy.wait_recv()
             near = start_near(sweep, acc)
-            own = start_own(sweep, outer_out)
             consts = [const_forward(1), const_forward(2)]
         elif not last:
             outs = start_source(sweep, outer_out)

time: 34.4 us -> 35.2 us (1.023)
  Pallas kernels: 33.6 us -> 34.4 us
    pallas_call x1, Pallas kernels: 33.6 us -> 34.4 us  [two_layers(): pl.pallas_call(functools.partial(two_layer_kernel, groups), out_shape=jax...]
where the time goes in v6:
time: 35.2 us; the launch traced here: 35.1 us
  Pallas kernels  34.4 us (98%)
  local copies, waits for them, and re-layouts  0.64 us (2%)
    pallas_call x1, Pallas kernels, two_layers(): pl.pallas_call(functools.partial(two_layer_kernel, groups), out_shape=jax...  34.4 us

profile of v6, /device:TPU:0, one launch (start us, length us, event | category | flops | bytes accessed | tf_op | source)
XLA Modules:
  0.0 35.1 jit_solution(15124227191486978450)
XLA Ops:
  0.0 34.4 %shard_map.91 = bf16[96,512]{1,0:T(8,128)(2,1)S(1)} custom-call(bf16[2048,512]{1,0:T(8,128)(2,1)} %bitcast.9, bf16[96,512]{1,0:T(8,128)(2,1)} %bitcast.10, s32[1,192]{1,0:T(1,128)} %bitcast.15, bf16[3,128,128]{2,1,0:T(8,128)(2,1)} %bitcast.11, bf16[128,128]{1,0:T(8,128)(2,1)} %bitcast.13, f32[1,128]{1,0:T(1,128)} %scale_hbm.1, s32[2]{0:T(128)} %counts_hbm.1, ...), custom_call_target="tpu_custom_call" | custom-call | tf_op jit(solution)/shard_map/pallas_call | solution.py:544
  34.4 0.6 %copy.11 = bf16[1,1,96,512]{3,2,1,0:T(8,128)(2,1)} copy(bf16[1,1,96,512]{3,2,1,0:T(8,128)(2,1)S(1)} %bitcast.8) | data formatting | bytes 196608
